TPU v7x, 512 devices: a whole 4x4x16 slice. The times are simulated.
512 devices in a mesh: cyc: 16 (over z), tile: 32 (over x, y, core).
Axes of the slice: x: 4, y: 4, z: 16, core: 2. Of those that a mesh axis runs over, the one named last changes fastest.
Arguments:
- weight_change: bfloat16 [16, 80, 80, 1024], P('cyc', None, None, 'tile'), may hold values from -0.1796875 to 0.1796875
- ensemble: bfloat16 [16, 80, 8, 16384], P('cyc', None, None, 'tile'), may hold values from -6 to 6
- stencil_index: int32 [4, 16384], P(None, 'tile'), may hold values from 0 to 39
- stencil_weight: float32 [4, 16384], P(None, 'tile'), may hold values from 0.1 to 1
Outputs:
- smoothed: bfloat16 [16, 80, 8, 16384], P('cyc', None, None, 'tile')
Inputs may be any that keep to these rules, and one draw needn't show every extreme that they name: `stencil_index`: positions 0 to 3 of the extended list are the last columns of the sector before (periodic in longitude), positions 36 and beyond the first columns of the sector after.
All inputs are finite; a program needn't handle non-finite values.
Results may differ from a plain program's by a relative error of at most 0.0085.
Values may be sent and summed in bfloat16 or wider, within the bound.
No kernel may reach another device: no remote copies, remote signals or barrier semaphores. Data moves between devices by JAX's collectives and lax.ppermute only.
A program may use at most 128 MiB of HBM per device.

v0:
```python
import math

import jax
import jax.numpy as jnp
from jax import lax
from jax.sharding import PartitionSpec as P

RIM_COLS = 4


def with_halo(block, sides, width):
    for axis, dim in sides:
        count = lax.axis_size(axis)
        forward = [(i, i + 1) for i in range(count - 1)]
        forward.append((count - 1, 0))
        backward = [(target, source) for source, target in forward]
        low = lax.ppermute(
            lax.slice_in_dim(block, block.shape[dim] - width, None, axis=dim), axis, forward
        )
        high = lax.ppermute(lax.slice_in_dim(block, 0, width, axis=dim), axis, backward)
        block = jnp.concatenate([low, block, high], axis=dim)
    return block


def combine(earlier, later):
    return jnp.einsum(
        "ijg,jkg->ikg",
        later,
        earlier,
        precision=lax.Precision.HIGHEST,
        preferred_element_type=jnp.float32,
    )


def suffix_of(raw, eye):
    mats = raw.astype(jnp.float32) + eye
    unity = jnp.broadcast_to(eye, mats.shape)
    every = lax.all_gather(raw[None], "cyc", axis=0, tiled=True)
    count = every.shape[0]
    mine = lax.axis_index("cyc")

    def step(number, carry):
        later_cycle = count - 1 - number
        weight = (
            lax.dynamic_index_in_dim(every, later_cycle, 0, keepdims=False).astype(jnp.float32)
            + eye
        )
        product = combine(carry, weight)
        return jnp.where(later_cycle > mine, product, carry)

    return lax.fori_loop(0, count, step, unity)


def on_device(weight_change, ensemble, stencil_index, stencil_weight):
    members = weight_change.shape[1]
    eye = jnp.eye(members, dtype=jnp.float32)[:, :, None]
    suffix = suffix_of(weight_change[0], eye)
    extended = with_halo(suffix, (("tile", 2),), RIM_COLS)
    width = extended.shape[2]
    flat = extended.reshape(members * members, width)
    shares = stencil_weight / jnp.sum(stencil_weight, axis=0, keepdims=True)
    states = ensemble[0]
    points = states.shape[2]
    block = math.gcd(points, 256)
    blocks = points // block
    slots = jnp.arange(width)[:, None]

    def one_block(number, output):
        begin = number * block
        index = lax.dynamic_slice_in_dim(stencil_index, begin, block, 1)
        weights = lax.dynamic_slice_in_dim(shares, begin, block, 1)
        table = jnp.zeros((width, block), jnp.float32)
        for corner in range(4):
            table = table + jnp.where(
                index[corner][None, :] == slots, weights[corner][None, :], 0.0
            )
        interp = jnp.dot(
            flat, table, precision=lax.Precision.HIGHEST, preferred_element_type=jnp.float32
        )
        interp = interp.reshape(members, members, block).astype(jnp.bfloat16)
        piece = lax.dynamic_slice_in_dim(states, begin, block, 2)
        mixed = jnp.einsum(
            "nvf,nmf->mvf", piece, interp, preferred_element_type=jnp.float32
        ).astype(jnp.bfloat16)
        return lax.dynamic_update_slice_in_dim(output, mixed, begin, 2)

    result = lax.fori_loop(0, blocks, one_block, jnp.zeros_like(states))
    return result[None]


def solution(mesh):
    placed = (
        P("cyc", None, None, "tile"),
        P("cyc", None, None, "tile"),
        P(None, "tile"),
        P(None, "tile"),
    )
    return jax.shard_map(
        on_device,
        mesh=mesh,
        in_specs=placed,
        out_specs=P("cyc", None, None, "tile"),
        check_vma=False,
    )
```

profile of v0, /device:TPU:31, one launch (start us, length us, event | category | flops | bytes accessed | tf_op | source)
XLA Modules:
  0.0 262.1 jit_solution(1129115053120165722)
XLA Ops:
  8.0 132.4 %all-gather.2.cloned.1.call-done = bf16[16,80,80,32]{2,3,1,0:T(8,128)(2,1)} async-done(((bf16[1,80,80,32]{2,3,1,0:T(8,128)(2,1)}), bf16[16,80,80,32]{2,3,1,0:T(8,128)(2,1)}) %all-gather.2.cloned.1.call-update) | async-done | bytes 6553616 | tf_op jit(solution)/shard_map/all_gather | solution.py:38
  140.5 48.1 %while.31 = (s32[]{:T(128)}, f32[80,80,32]{1,0,2:T(8,128)S(1)}, s32[]{:T(128)}, bf16[16,80,80,32]{2,3,1,0:T(8,128)(2,1)}, s32[]{:T(128)}, /*index=5*/s32[]{:T(128)}, s32[]{:T(128)}, s32[]{:T(128)}) while((s32[]{:T(128)}, f32[80,80,32]{1,0,2:T(8,128)S(1)}, s32[]{:T(128)}, bf16[16,80,80,32]{2,3,1,0:T(8,128)(2,1)}, s32[]{:T(128)}, ...), condition=%wide.region_2.3_spmd.clone, body=%wide.region_1.2_spmd.clone.sunk | while | flops 197235200 | bytes 4556945 | solution.py:51
  141.8 1.7 fusion.41
  144.8 1.7 fusion.41
  147.8 1.7 fusion.41
  150.8 1.7 fusion.41
  153.8 1.7 fusion.41
  156.8 1.7 fusion.41
  159.8 1.7 fusion.41
  162.8 1.7 fusion.41
  165.8 1.7 fusion.41
  168.8 1.7 fusion.41
  171.8 1.7 fusion.41
  174.8 1.7 fusion.41
  177.8 1.7 fusion.41
  180.8 1.7 fusion.41
  183.8 1.7 fusion.41
  186.8 1.7 fusion.41
  188.6 2.8 %collective-permute-start = (f32[80,80,4]{1,0,2:T(8,128)S(1)}, f32[80,80,4]{1,0,2:T(8,128)S(1)}, u32[]{:S(2)}, u32[]{:S(2)}) collective-permute-start(f32[80,80,4]{1,0,2:T(8,128)S(1)} %get-tuple-element.348), channel_id=1, source_target_pairs={{0,1},{1,2},{2,3},{3,4},{4,5},{5,6},{6,7},{7,8},{8,9},{9,10},{10,1... | collective-permute-start | bytes 307208 | tf_op jit(solution)/shard_map/ppermute | solution.py:17
  191.5 1.9 collective-permute-start.1
  193.4 1.7 copy.19
  195.2 6.2 %collective-permute-done.1 = f32[80,80,4]{1,0,2:T(8,128)S(1)} collective-permute-done((f32[80,80,4]{1,0,2:T(8,128)S(1)}, f32[80,80,4]{1,0,2:T(8,128)S(1)}, u32[]{:S(2)}, u32[]{:S(2)}) %collective-permute-start.1) | collective-permute-done | bytes 102432 | tf_op jit(solution)/shard_map/ppermute | solution.py:20
  201.5 2.4 copy.18
  204.8 50.4 %while.32 = (s32[]{:T(128)}, bf16[80,8,512]{2,1,0:T(8,128)(2,1)}, s32[4,512]{1,0:T(4,128)S(1)}, f32[4,512]{1,0:T(4,128)S(1)}, f32[6400,40]{1,0:T(8,128)}, /*inde...) while((s32[]{:T(128)}, bf16[80,8,512]{2,1,0:T(8,128)(2,1)}, ...), condition=%wide.region_4.5_spmd.clone.clone, body=%wide.region_3.4_spmd.clone.clone.sunk | while | flops 814561280 | bytes 30736716 | solution.py:87
  205.0 8.2 %fusion.46 = bf16[6400,256]{0,1:T(8,128)(2,1)S(1)} fusion(f32[6400,40]{1,0:T(8,128)} %get-tuple-element.482, f32[256]{0:T(256)S(1)} %bitcast.71, s32[256]{0:T(256)S(1)} %bitcast.75, f32[256]{0:T(256)S(1)} %bitcast.69, s32[256]{0:T(256)S(1)} %bitcast.73, f32[256]{0:T(256)S(1)} %bitcast.70, s32[256]{0:T(256)S(1)} %bitcast.74, f32[256]{0:T(256)S(1)} %bitcast.68, ...), kind=kOutput, calls=%fused_computation.11.clone.1 | convolution fusion | flops 788183040 | bytes 4308992 | tf_op jit(solution)/shard_map/while/body/eval_jaxpr/dot_general | solution.py:77
  213.1 3.5 %copy.33 = bf16[6400,256]{1,0:T(8,128)(2,1)} copy(bf16[6400,256]{0,1:T(8,128)(2,1)S(1)} %fusion.46) | data formatting | bytes 6553600 | tf_op jit(solution)/shard_map/while/body/eval_jaxpr/convert_element_type | solution.py:80
  216.6 8.0 %copy.34 = bf16[80,80,256]{1,0,2:T(8,128)(2,1)} copy(bf16[80,80,256]{2,1,0:T(8,128)(2,1)} %bitcast.65) | data formatting | bytes 6553600 | tf_op jit(solution)/shard_map/while/body/eval_jaxpr/convert_element_type | solution.py:80
  224.6 4.0 %fusion.47 = bf16[80,8,256]{0,1,2:T(8,128)(2,1)S(1)} fusion(bf16[80,80,256]{1,0,2:T(8,128)(2,1)} %copy.34, bf16[80,8,512]{0,1,2:T(8,128)(2,1)S(1)} %copy-done, s32[]{:T(128)S(6)} %select_n.118), kind=kOutput, calls=%fused_computation.13.clone.1 | convolution fusion | flops 26378240 | bytes 4128772 | tf_op jit(solution)/shard_map/while/body/eval_jaxpr/nvf,nmf->mvf/dot_general | solution.py:82
  230.2 8.2 %fusion.46 = bf16[6400,256]{0,1:T(8,128)(2,1)S(1)} fusion(f32[6400,40]{1,0:T(8,128)} %get-tuple-element.482, f32[256]{0:T(256)S(1)} %bitcast.71, s32[256]{0:T(256)S(1)} %bitcast.75, f32[256]{0:T(256)S(1)} %bitcast.69, s32[256]{0:T(256)S(1)} %bitcast.73, f32[256]{0:T(256)S(1)} %bitcast.70, s32[256]{0:T(256)S(1)} %bitcast.74, f32[256]{0:T(256)S(1)} %bitcast.68, ...), kind=kOutput, calls=%fused_computation.11.clone.1 | convolution fusion | flops 788183040 | bytes 4308992 | tf_op jit(solution)/shard_map/while/body/eval_jaxpr/dot_general | solution.py:77
  238.4 3.5 %copy.33 = bf16[6400,256]{1,0:T(8,128)(2,1)} copy(bf16[6400,256]{0,1:T(8,128)(2,1)S(1)} %fusion.46) | data formatting | bytes 6553600 | tf_op jit(solution)/shard_map/while/body/eval_jaxpr/convert_element_type | solution.py:80
  241.8 8.0 %copy.34 = bf16[80,80,256]{1,0,2:T(8,128)(2,1)} copy(bf16[80,80,256]{2,1,0:T(8,128)(2,1)} %bitcast.65) | data formatting | bytes 6553600 | tf_op jit(solution)/shard_map/while/body/eval_jaxpr/convert_element_type | solution.py:80
  249.8 4.0 %fusion.47 = bf16[80,8,256]{0,1,2:T(8,128)(2,1)S(1)} fusion(bf16[80,80,256]{1,0,2:T(8,128)(2,1)} %copy.34, bf16[80,8,512]{0,1,2:T(8,128)(2,1)S(1)} %copy-done, s32[]{:T(128)S(6)} %select_n.118), kind=kOutput, calls=%fused_computation.13.clone.1 | convolution fusion | flops 26378240 | bytes 4128772 | tf_op jit(solution)/shard_map/while/body/eval_jaxpr/nvf,nmf->mvf/dot_general | solution.py:82
  (84 shorter events, 25.3 us)
Async XLA Ops:
  6.5 133.8 %all-gather.2.cloned.1.call-start = ((), (), s32[]{:S(2)}) async-start(), calls=%async_computation | async-start | bytes 11141120 | tf_op jit(solution)/shard_map/all_gather | solution.py:38
  140.4 52.9 %copy-start.5 = (f32[4,512]{1,0:T(4,128)S(1)}, f32[4,512]{1,0:T(4,128)}, u32[]{:S(2)}) copy-start(f32[4,512]{1,0:T(4,128)} %param.11) | copy-start | bytes 24580
  140.5 53.0 %copy-start.1 = (bf16[1,80,8,512]{3,2,1,0:T(8,128)(2,1)S(1)}, bf16[1,80,8,512]{3,2,1,0:T(8,128)(2,1)}, u32[]{:S(2)}) copy-start(bf16[1,80,8,512]{3,2,1,0:T(8,128)(2,1)} %param.9) | copy-start | bytes 1966084
  188.6 6.6 %collective-permute-start = (f32[80,80,4]{1,0,2:T(8,128)S(1)}, f32[80,80,4]{1,0,2:T(8,128)S(1)}, u32[]{:S(2)}, u32[]{:S(2)}) collective-permute-start(f32[80,80,4]{1,0,2:T(8,128)S(1)} %get-tuple-element.348), channel_id=1, source_target_pairs={{0,1},{1,2},{2,3},{3,4},{4,5},{5,6},{6,7},{7,8},{8,9},{9,10},{10,1... | collective-permute-start | bytes 307208 | tf_op jit(solution)/shard_map/ppermute | solution.py:17
  191.5 10.0 %collective-permute-start.1 = (f32[80,80,4]{1,0,2:T(8,128)S(1)}, f32[80,80,4]{1,0,2:T(8,128)S(1)}, u32[]{:S(2)}, u32[]{:S(2)}) collective-permute-start(f32[80,80,4]{1,0,2:T(8,128)S(1)} %get-tuple-element.349), channel_id=1, source_target_pairs={{1,0},{2,1},{3,2},{4,3},{5,4},{6,5},{7,6},{8,7},{9,8},{10,9},{11,1... | collective-permute-start | bytes 307208 | tf_op jit(solution)/shard_map/ppermute | solution.py:20
  201.5 3.3 %copy-start.4 = (s32[4,512]{1,0:T(4,128)S(1)}, s32[4,512]{1,0:T(4,128)}, u32[]{:S(2)}) copy-start(s32[4,512]{1,0:T(4,128)} %param.10) | copy-start | bytes 24580
  216.6 8.0 %copy-start = (bf16[80,8,512]{0,1,2:T(8,128)(2,1)S(1)}, bf16[80,8,512]{0,1,2:T(8,128)(2,1)}, u32[]{:S(2)}) copy-start(bf16[80,8,512]{0,1,2:T(8,128)(2,1)} %get-tuple-element.483) | copy-start | bytes 1966084 | tf_op jit(solution)/shard_map/while
  224.6 4.5 %copy-start.2 = (bf16[80,8,512]{2,1,0:T(8,128)(2,1)S(1)}, bf16[80,8,512]{2,1,0:T(8,128)(2,1)}, u32[]{:S(2)}) copy-start(bf16[80,8,512]{2,1,0:T(8,128)(2,1)} %get-tuple-element.466) | copy-start | bytes 1966084 | tf_op jit(solution)/shard_map/while
  229.2 0.8 copy-start.3
  241.8 8.0 %copy-start = (bf16[80,8,512]{0,1,2:T(8,128)(2,1)S(1)}, bf16[80,8,512]{0,1,2:T(8,128)(2,1)}, u32[]{:S(2)}) copy-start(bf16[80,8,512]{0,1,2:T(8,128)(2,1)} %get-tuple-element.483) | copy-start | bytes 1966084 | tf_op jit(solution)/shard_map/while
  249.8 4.5 %copy-start.2 = (bf16[80,8,512]{2,1,0:T(8,128)(2,1)S(1)}, bf16[80,8,512]{2,1,0:T(8,128)(2,1)}, u32[]{:S(2)}) copy-start(bf16[80,8,512]{2,1,0:T(8,128)(2,1)} %get-tuple-element.466) | copy-start | bytes 1966084 | tf_op jit(solution)/shard_map/while
  254.4 0.8 copy-start.3
Sparse Core Ops, SparseCore 0:
  9.4 130.8 all-gather.1
where the time goes:
time: 263 us; the launch traced here: 262 us
  waiting for transfers between devices  139 us (53%)
  matrix products  52 us (20%)
  local copies, waits for them, and re-layouts  50.7 us (19%)
  between operations  13.5 us (5%)
  starting transfers between devices  4.75 us (2%)
    all_gather x1, waiting for transfers between devices, suffix_of(): every = lax.all_gather(raw[None], 'cyc', axis=0, tiled=True)  132 us
    dot_general x16, matrix products, combine(): jnp.einsum('ijg,jkg->ikg', later, earlier, precision=lax.Precision.HIGHES...  27.6 us
    convert_element_type x4, local copies, waits for them, and re-layouts, one_block(): interp = interp.reshape(members, members, block).astype(jnp.bfloat16)  22.9 us
    dynamic_slice x16, local copies, waits for them, and re-layouts, step(): lax.dynamic_index_in_dim(every, later_cycle, 0, keepdims=False)  18.2 us
    dot_general x2, matrix products, one_block(): jnp.dot(flat, table, precision=lax.Precision.HIGHEST, preferred_element_t...  16.4 us
    dot_general x2, matrix products, one_block(): jnp.einsum('nvf,nmf->mvf', piece, interp, preferred_element_type=jnp.floa...  8.02 us
    ppermute x1, waiting for transfers between devices, with_halo(): lax.ppermute(lax.slice_in_dim(block, 0, width, axis=dim), axis, backward)  6.25 us
  transfers between devices with their start and end apart: 3, of which 2 were waited for; matrix products, arithmetic and copies ran while one was open for 1% of the time, Pallas kernels for 0%

commit v1 on v0

v1 whole, which is shorter than its diff:
```python
import jax
import jax.numpy as jnp
from jax import lax
from jax.experimental import pallas as pl
from jax.experimental.pallas import tpu as pltpu
from jax.sharding import PartitionSpec as P

RIM = 4
LANES = 128
SPAN = 4
NEAR = [[SPAN * k + r for r in range(SPAN)] for k in range(SPAN)]
FAR = [[SPAN * k + r for k in range(SPAN)] for r in range(SPAN)]
F32 = jnp.float32
BF16 = jnp.bfloat16


def mm(a, b):
    return jnp.dot(a, b, preferred_element_type=F32)


def mm_split(a, b):
    high = a.astype(BF16)
    low = (a - high.astype(F32)).astype(BF16)
    return mm(high, b) + mm(low, b)


def part(array, g, n):
    return array[:, g * n : (g + 1) * n]


def pack_kernel(x_ref, out_ref, rows):
    n, cols, _ = x_ref.shape
    per = cols // SPAN
    for i in range(n):
        rows[i * cols : (i + 1) * cols, :n] = x_ref[i].astype(F32)
    for q in range(SPAN):
        mats = [rows[pl.ds(q * per + g, n, stride=cols), :].T[:n] for g in range(per)]
        out_ref[q] = jnp.concatenate(mats, axis=1).astype(BF16)


def near_kernel(d_ref, e_ref, g_ref):
    n = d_ref.shape[1]
    per = d_ref.shape[2] // n
    d = [d_ref[r] for r in range(SPAN)]
    e0s, e1s, gs = [], [], []
    for g in range(per):
        d0, d1, d2, d3 = [part(a, g, n) for a in d]
        e1 = d3.astype(F32) + d2.astype(F32) + mm(d3, d2)
        e0 = e1 + d1.astype(F32) + mm_split(e1, d1)
        whole = e0 + d0.astype(F32) + mm_split(e0, d0)
        e0s.append(e0)
        e1s.append(e1)
        gs.append(whole)
    e_ref[0] = jnp.concatenate(e0s, axis=1)
    e_ref[1] = jnp.concatenate(e1s, axis=1)
    e_ref[2] = d[3].astype(F32)
    g_ref[...] = jnp.concatenate(gs, axis=1).astype(BF16)


def far_kernel(mine_ref, w_ref, e_ref, out_ref):
    n = w_ref.shape[1]
    per = w_ref.shape[2] // n
    mine = mine_ref[0]
    h = [w_ref[k] * jnp.where(mine < k, 1.0, 0.0).astype(BF16) for k in range(SPAN)]
    e = [e_ref[r] for r in range(SPAN - 1)]
    outs = [[] for _ in range(SPAN)]
    for g in range(per):
        _, h1, h2, h3 = [part(a, g, n) for a in h]
        s = h3.astype(F32) + h2.astype(F32) + mm(h3, h2)
        s = s + h1.astype(F32) + mm_split(s, h1)
        for r in range(SPAN - 1):
            er = part(e[r], g, n)
            outs[r].append(s + er + mm_split(s, er.astype(BF16)))
        outs[SPAN - 1].append(s)
    for r in range(SPAN):
        out_ref[r] = jnp.concatenate(outs[r], axis=1).astype(BF16)


def table_of(index_ref, weight_ref, slots):
    weight = weight_ref[...]
    share = weight / jnp.sum(weight, axis=0, keepdims=True)
    index = index_ref[...]
    points = index.shape[1]
    row = lax.broadcasted_iota(jnp.int32, (slots, points), 0)
    table = jnp.zeros((slots, points), F32)
    for j in range(4):
        table = table + jnp.where(index[j][None, :] == row, share[j][None, :], 0.0)
    return table


def apply_kernel(index_ref, weight_ref, x_ref, p_ref, low_ref, high_ref, out_ref, rows, tall):
    n, channels, points = x_ref.shape
    chunks = p_ref.shape[0]
    per = p_ref.shape[2] // n
    slots = chunks * per + 2 * RIM
    wide = points // LANES
    for i in range(n):
        for t in range(wide):
            rows[t, i * channels : (i + 1) * channels, :] = x_ref[i, :, t * LANES : (t + 1) * LANES].astype(F32)
    table = table_of(index_ref, weight_ref, slots)
    for g in range(slots):
        tall[g] = jnp.broadcast_to(table[g][None, :], (16, points)).astype(BF16)

    def channel(v, carry):
        at = pl.ds(v, n, stride=channels)
        state = jnp.concatenate([rows[t, at, :] for t in range(wide)], axis=1)
        x = state.astype(BF16).reshape(n // 16, 16, points)

        def scaled(slot):
            return (x * tall[slot][None]).reshape(n, points)

        acc = state
        for i in range(chunks):
            many = jnp.concatenate([scaled(RIM + i * per + g) for g in range(per)], axis=0)
            acc = acc + mm(p_ref[i], many)
        many = jnp.concatenate([scaled(g) for g in range(RIM)], axis=0)
        acc = acc + mm(low_ref[...], many)
        many = jnp.concatenate([scaled(RIM + chunks * per + g) for g in range(RIM)], axis=0)
        acc = acc + mm(high_ref[...], many)
        for t in range(wide):
            rows[t, at, :] = acc[:, t * LANES : (t + 1) * LANES]
        return carry

    lax.fori_loop(0, channels, channel, 0)
    for i in range(n):
        for t in range(wide):
            out_ref[i, :, t * LANES : (t + 1) * LANES] = rows[t, i * channels : (i + 1) * channels, :].astype(BF16)


def call(body, outs, scratch=(), inputs=0, scalars=0, name=None):
    vmem = pl.BlockSpec(memory_space=pltpu.VMEM)
    smem = pl.BlockSpec(memory_space=pltpu.SMEM)
    return pl.pallas_call(
        body,
        out_shape=outs,
        in_specs=[smem] * scalars + [vmem] * inputs,
        out_specs=jax.tree.map(lambda _: vmem, outs),
        scratch_shapes=list(scratch),
        compiler_params=pltpu.CompilerParams(vmem_limit_bytes=56 * 1024 * 1024),
        name=name,
    )


def on_device(weight_change, ensemble, stencil_index, stencil_weight):
    _, n, _, cols = weight_change.shape
    per = cols // SPAN
    lanes = per * n
    chunk = jax.ShapeDtypeStruct((SPAN, n, lanes), BF16)
    raw = jnp.transpose(weight_change[0], (0, 2, 1))
    states = ensemble[0]
    points = states.shape[2]

    packed = call(pack_kernel, chunk, [pltpu.VMEM((n * cols, LANES), F32)], inputs=1, name="pack")(raw)
    mine = lax.all_to_all(packed, "cyc", 0, 0, axis_index_groups=NEAR, tiled=True)
    near, whole = call(
        near_kernel,
        (jax.ShapeDtypeStruct((SPAN - 1, n, lanes), F32), jax.ShapeDtypeStruct((n, lanes), BF16)),
        inputs=1,
        name="near",
    )(mine)
    wholes = lax.all_gather(whole, "cyc", axis=0, axis_index_groups=FAR)
    group = (lax.axis_index("cyc") // SPAN).astype(jnp.int32).reshape(1)
    sent = call(far_kernel, chunk, inputs=2, scalars=1, name="far")(group, wholes, near)
    suffix = lax.all_to_all(sent, "cyc", 0, 0, axis_index_groups=NEAR, tiled=True)

    count = lax.axis_size("tile")
    forward = [(i, (i + 1) % count) for i in range(count)]
    backward = [(target, source) for source, target in forward]
    low = lax.ppermute(suffix[SPAN - 1, :, lanes - RIM * n :], "tile", forward)
    high = lax.ppermute(suffix[0, :, : RIM * n], "tile", backward)
    slots = cols + 2 * RIM
    result = call(
        apply_kernel,
        jax.ShapeDtypeStruct(states.shape, BF16),
        [pltpu.VMEM((points // LANES, n * states.shape[1], LANES), F32), pltpu.VMEM((slots, 16, points), BF16)],
        inputs=6,
        name="apply",
    )(stencil_index, stencil_weight, states, suffix, low, high)
    return result[None]


def solution(mesh):
    placed = (
        P("cyc", None, None, "tile"),
        P("cyc", None, None, "tile"),
        P(None, "tile"),
        P(None, "tile"),
    )
    return jax.shard_map(
        on_device,
        mesh=mesh,
        in_specs=placed,
        out_specs=P("cyc", None, None, "tile"),
        check_vma=False,
    )
```

time: 263 us -> 92.6 us (0.35)
  the two profiles are of different devices: /device:TPU:31 before, /device:TPU:32 now
where the time goes in v1:
time: 92.6 us; the launch traced here: 92.2 us
  blocking collectives  40.8 us (44%)
  Pallas kernels  22.1 us (24%)
  waiting for transfers between devices  14.5 us (16%)
  starting transfers between devices  13.3 us (14%)
  local copies, waits for them, and re-layouts  1.46 us (2%)
    all_gather x1, blocking collectives, on_device(): wholes = lax.all_gather(whole, 'cyc', axis=0, axis_index_groups=FAR)  27.2 us
    all_to_all x1, blocking collectives, on_device(): lax.all_to_all(sent, 'cyc', 0, 0, axis_index_groups=NEAR, tiled=True)  13.6 us
    all_to_all x1, starting transfers between devices, on_device(): lax.all_to_all(packed, 'cyc', 0, 0, axis_index_groups=NEAR, tiled=True)  8.88 us
    pallas_call x1, Pallas kernels, on_device(): call(apply_kernel, jax.ShapeDtypeStruct(states.shape, BF16), [pltpu.VMEM(...  8.7 us
    all_to_all x1, waiting for transfers between devices, on_device(): lax.all_to_all(packed, 'cyc', 0, 0, axis_index_groups=NEAR, tiled=True)  7.55 us
    ppermute x1, waiting for transfers between devices, on_device(): low = lax.ppermute(suffix[SPAN - 1, :, lanes - RIM * n:], 'tile', forward)  6.91 us
    pallas_call x1, Pallas kernels, on_device(): call(far_kernel, chunk, inputs=2, scalars=1, name='far')  5.62 us
    pallas_call x1, Pallas kernels, on_device(): call(near_kernel, (jax.ShapeDtypeStruct((SPAN - 1, n, lanes), F32), jax.S...  4.87 us
  transfers between devices with their start and end apart: 3, of which 2 were waited for; matrix products, arithmetic and copies ran while one was open for 0% of the time, Pallas kernels for 0%

profile of v1, /device:TPU:32, one launch (start us, length us, event | category | flops | bytes accessed | tf_op | source)
XLA Modules:
  0.0 92.2 jit_solution(11813934710410368707)
XLA Ops:
  0.0 2.9 %pack.1 = bf16[4,80,640]{2,1,0:T(8,128)(2,1)} custom-call(bf16[80,32,80]{2,1,0:T(8,128)(2,1)} %bitcast.13), custom_call_target="tpu_custom_call" | custom-call | tf_op jit(solution)/shard_map/pack/pallas_call | solution.py:153
  2.9 8.9 %all-to-all-start = ((bf16[4,80,640]{2,1,0:T(8,128)(2,1)}), bf16[4,80,640]{2,1,0:T(8,128)(2,1)S(1)}, u32[]{:S(2)}, u32[]{:S(2)}) async-start(bf16[4,80,640]{2,1,0:T(8,128)(2,1)} %pack.1), calls=%async_computation | async-start | bytes 819200 | tf_op jit(solution)/shard_map/all_to_all | solution.py:154
  11.8 7.6 %all-to-all-done.d_ref = bf16[4,80,640]{2,1,0:T(8,128)(2,1)S(1)} async-done(((bf16[4,80,640]{2,1,0:T(8,128)(2,1)}), bf16[4,80,640]{2,1,0:T(8,128)(2,1)S(1)}, u32[]{:S(2)}, u32[]{:S(2)}) %all-to-all-start) | async-done | bytes 409632 | tf_op jit(solution)/shard_map/all_to_all | solution.py:154
  19.3 0.0 copy-start.1
  19.3 0.8 copy-done.1
  20.1 4.9 %near.1 = (f32[3,80,640]{2,1,0:T(8,128)}, bf16[80,640]{1,0:T(8,128)(2,1)}) custom-call(bf16[4,80,640]{2,1,0:T(8,128)(2,1)} %copy-done.1), custom_call_target="tpu_custom_call" | custom-call | tf_op jit(solution)/shard_map/near/pallas_call | solution.py:155
  24.9 27.2 %all-gather = bf16[320,640]{1,0:T(8,128)(2,1)} all-gather(bf16[80,640]{1,0:T(8,128)(2,1)} %get-tuple-element.7), channel_id=2, replica_groups={{0,128,256,384},{32,160,288,416},{64,192,320,448},{96,224,352,480},{1,1..., dimensions={0}, use_global_device_ids=true | all-gather | bytes 512000 | tf_op jit(solution)/shard_map/all_gather | solution.py:161
  52.2 5.6 %far.1 = bf16[4,80,640]{2,1,0:T(8,128)(2,1)} custom-call(s32[1]{0:T(128)} %bitcast.1.mine_ref, bf16[4,80,640]{2,1,0:T(8,128)(2,1)} %bitcast.11, f32[3,80,640]{2,1,0:T(8,128)} %get-tuple-element.8.e_ref), custom_call_target="tpu_custom_call" | custom-call | tf_op jit(solution)/shard_map/far/pallas_call | solution.py:163
  57.8 13.6 %all_to_all.10.p_ref = bf16[4,80,640]{2,1,0:T(8,128)(2,1)S(1)} all-to-all(bf16[4,80,640]{2,1,0:T(8,128)(2,1)} %far.1), channel_id=1, replica_groups={{0,32,64,96},{128,160,192,224},{256,288,320,352},{384,416,448,480},{1,3..., dimensions={0} | all-to-all | bytes 819200 | tf_op jit(solution)/shard_map/all_to_all | solution.py:164
  71.4 0.0 copy-start
  71.4 0.1 slice_bitcast_fusion
  71.5 2.5 %collective-permute-start.1 = (bf16[80,320]{1,0:T(8,128)(2,1)S(1)}, bf16[80,320]{1,0:T(8,128)(2,1)S(1)}, u32[]{:S(2)}, u32[]{:S(2)}) collective-permute-start(bf16[80,320]{1,0:T(8,128)(2,1)S(1)} %get-tuple-element.9), channel_id=1, source_target_pairs={{1,0},{2,1},{3,2},{4,3},{5,4},{6,5},{7,6},{8,7},{9,8},{10,9},{11,1... | collective-permute-start | bytes 153608 | tf_op jit(solution)/shard_map/ppermute | solution.py:170
  74.0 1.9 %collective-permute-start = (bf16[80,320]{1,0:T(8,128)(2,1)S(1)}, bf16[80,320]{1,0:T(8,128)(2,1)S(1)}, u32[]{:S(2)}, u32[]{:S(2)}) collective-permute-start(bf16[80,320]{1,0:T(8,128)(2,1)S(1)} %get-tuple-element.10), channel_id=1, source_target_pairs={{0,1},{1,2},{2,3},{3,4},{4,5},{5,6},{6,7},{7,8},{8,9},{9,10},{10,1... | collective-permute-start | bytes 153608 | tf_op jit(solution)/shard_map/ppermute | solution.py:169
  75.9 0.0 collective-permute-done.1.high_ref
  75.9 0.0 copy-start.2
  75.9 6.9 %collective-permute-done.low_ref = bf16[80,320]{1,0:T(8,128)(2,1)S(1)} collective-permute-done((bf16[80,320]{1,0:T(8,128)(2,1)S(1)}, bf16[80,320]{1,0:T(8,128)(2,1)S(1)}, u32[]{:S(2)}, u32[]{:S(2)}) %collective-permute-start) | collective-permute-done | bytes 51232 | tf_op jit(solution)/shard_map/ppermute | solution.py:169
  82.8 0.0 copy-start.3
  82.8 0.0 copy-done
  82.8 0.0 copy-done.2
  82.8 0.6 copy-done.3
  83.5 8.7 %apply.1 = bf16[80,8,512]{2,1,0:T(8,128)(2,1)} custom-call(s32[4,512]{1,0:T(4,128)} %index_ref.1, f32[4,512]{1,0:T(4,128)} %weight_ref.1, bf16[80,8,512]{2,1,0:T(8,128)(2,1)} %bitcast.12, bf16[4,80,640]{2,1,0:T(8,128)(2,1)} %copy-done, bf16[80,320]{1,0:T(8,128)(2,1)} %copy-done.3, bf16[80,320]{1,0:T(8,128)(2,1)} %copy-done.2), custom_call_target="tpu_custom_call" | custom-call | tf_op jit(solution)/shard_map/apply/pallas_call | solution.py:172
Async XLA Ops:
  2.9 16.4 %all-to-all-start = ((bf16[4,80,640]{2,1,0:T(8,128)(2,1)}), bf16[4,80,640]{2,1,0:T(8,128)(2,1)S(1)}, u32[]{:S(2)}, u32[]{:S(2)}) async-start(bf16[4,80,640]{2,1,0:T(8,128)(2,1)} %pack.1), calls=%async_computation | async-start | bytes 819200 | tf_op jit(solution)/shard_map/all_to_all | solution.py:154
  19.3 0.8 copy-start.1
  71.4 11.5 %copy-start = (bf16[4,80,640]{2,1,0:T(8,128)(2,1)}, bf16[4,80,640]{2,1,0:T(8,128)(2,1)S(1)}, u32[]{:S(2)}) copy-start(bf16[4,80,640]{2,1,0:T(8,128)(2,1)S(1)} %all_to_all.10.p_ref) | copy-start | bytes 1228804
  71.5 4.5 %collective-permute-start.1 = (bf16[80,320]{1,0:T(8,128)(2,1)S(1)}, bf16[80,320]{1,0:T(8,128)(2,1)S(1)}, u32[]{:S(2)}, u32[]{:S(2)}) collective-permute-start(bf16[80,320]{1,0:T(8,128)(2,1)S(1)} %get-tuple-element.9), channel_id=1, source_target_pairs={{1,0},{2,1},{3,2},{4,3},{5,4},{6,5},{7,6},{8,7},{9,8},{10,9},{11,1... | collective-permute-start | bytes 153608 | tf_op jit(solution)/shard_map/ppermute | solution.py:170
  74.0 8.9 %collective-permute-start = (bf16[80,320]{1,0:T(8,128)(2,1)S(1)}, bf16[80,320]{1,0:T(8,128)(2,1)S(1)}, u32[]{:S(2)}, u32[]{:S(2)}) collective-permute-start(bf16[80,320]{1,0:T(8,128)(2,1)S(1)} %get-tuple-element.10), channel_id=1, source_target_pairs={{0,1},{1,2},{2,3},{3,4},{4,5},{5,6},{6,7},{7,8},{8,9},{9,10},{10,1... | collective-permute-start | bytes 153608 | tf_op jit(solution)/shard_map/ppermute | solution.py:169
  75.9 6.9 %copy-start.2 = (bf16[80,320]{1,0:T(8,128)(2,1)}, bf16[80,320]{1,0:T(8,128)(2,1)S(1)}, u32[]{:S(2)}) copy-start(bf16[80,320]{1,0:T(8,128)(2,1)S(1)} %collective-permute-done.1.high_ref) | copy-start | bytes 153604
  82.8 0.6 copy-start.3

commit v2 on v1

v2 whole, which is shorter than its diff:
```python
import jax
import jax.numpy as jnp
from jax import lax
from jax.experimental import pallas as pl
from jax.experimental.pallas import tpu as pltpu
from jax.sharding import PartitionSpec as P

RIM = 4
LANES = 128
SPAN = 4
NEAR = [[SPAN * k + r for r in range(SPAN)] for k in range(SPAN)]
FAR = [[SPAN * k + r for k in range(SPAN)] for r in range(SPAN)]
F32 = jnp.float32
BF16 = jnp.bfloat16


def mm(a, b):
    return jnp.dot(a, b, preferred_element_type=F32)


def halves(a):
    high = a.astype(BF16)
    low = (a - high.astype(F32)).astype(BF16)
    return jnp.concatenate([high, low], axis=0)


def product(a, b):
    n, lanes = b.shape
    block = lax.broadcasted_iota(jnp.int32, (1, lanes), 1) // n
    rows = [jnp.where(block == g, b, jnp.zeros_like(b)) for g in range(lanes // n)]
    square = jnp.concatenate(rows, axis=0)
    outs = []
    for begin in range(0, lanes, 2 * LANES):
        end = min(lanes, begin + 2 * LANES)
        first = begin // n * n // LANES * LANES
        last = min(lanes, -(-(-(-end // n) * n) // LANES) * LANES)
        outs.append(mm(a[:, first:last], square[first:last, begin:end]))
    return jnp.concatenate(outs, axis=1)


def joined(a, b):
    n = b.shape[0]
    both = product(halves(a), b)
    return a + b.astype(F32) + both[:n] + both[n:]


def pack_kernel(x_ref, out_ref, rows):
    n, cols, _ = x_ref.shape
    per = cols // SPAN
    for i in range(n):
        rows[i * cols : (i + 1) * cols, :n] = x_ref[i].astype(F32)
    for q in range(SPAN):
        mats = [rows[pl.ds(q * per + g, n, stride=cols), :].T[:n] for g in range(per)]
        out_ref[q] = jnp.concatenate(mats, axis=1).astype(BF16)


def near_kernel(d_ref, e_ref, g_ref):
    d0, d1, d2, d3 = [d_ref[r] for r in range(SPAN)]
    e1 = d3.astype(F32) + d2.astype(F32) + product(d3, d2)
    e0 = joined(e1, d1)
    e_ref[0] = e0.astype(BF16)
    e_ref[1] = e1.astype(BF16)
    e_ref[2] = d3
    g_ref[...] = joined(e0, d0).astype(BF16)


def far_kernel(mine_ref, w_ref, e_ref, out_ref, own_ref, made, sems):
    mine = mine_ref[0]
    place = mine_ref[1]
    _, h1, h2, h3 = [w_ref[k] * jnp.where(mine < k, 1.0, 0.0).astype(BF16) for k in range(SPAN)]
    s = joined(h3.astype(F32) + h2.astype(F32) + product(h3, h2), h1)
    n = s.shape[0]
    parts = halves(s)
    copies = [pltpu.make_async_copy(made.at[r], out_ref.at[r], sems.at[r]) for r in range(SPAN)]
    made[SPAN - 1] = s.astype(BF16)
    copies[SPAN - 1].start()
    for r in range(SPAN - 1):
        e = e_ref[r]
        both = product(parts, e)
        made[r] = (s + e.astype(F32) + both[:n] + both[n:]).astype(BF16)
        copies[r].start()
    own_ref[...] = made[place]
    for copy in copies:
        copy.wait()


def table_of(index_ref, weight_ref, slots):
    weight = weight_ref[...]
    share = weight / jnp.sum(weight, axis=0, keepdims=True)
    index = index_ref[...]
    points = index.shape[1]
    row = lax.broadcasted_iota(jnp.int32, (slots, points), 0)
    table = jnp.zeros((slots, points), F32)
    for j in range(4):
        table = table + jnp.where(index[j][None, :] == row, share[j][None, :], 0.0)
    return table


def ready_kernel(index_ref, weight_ref, x_ref, states_ref, tall_ref, rows):
    n, channels, points = x_ref.shape
    wide = points // LANES
    for i in range(n):
        for t in range(wide):
            rows[t, i * channels : (i + 1) * channels, :] = x_ref[i, :, t * LANES : (t + 1) * LANES].astype(F32)
    for v in range(channels):
        for t in range(wide):
            states_ref[v, :, t * LANES : (t + 1) * LANES] = rows[t, pl.ds(v, n, stride=channels), :].astype(BF16)
    slots = tall_ref.shape[0]
    table = table_of(index_ref, weight_ref, slots)
    for g in range(slots):
        tall_ref[g] = jnp.broadcast_to(table[g][None, :], (16, points)).astype(BF16)


def mixed(states_ref, tall_ref, v, matrices, slots, begin=0, points=None):
    _, n, whole = states_ref.shape
    points = points or whole
    at = slice(begin, begin + points)
    x = states_ref[v, :, at].reshape(n // 16, 16, points)
    many = jnp.concatenate([(x * tall_ref[slot, :, at][None]).reshape(n, points) for slot in slots], axis=0)
    return mm(matrices, many)


def own_kernel(mine_ref, p_ref, states_ref, tall_ref, out_ref):
    channels, n, _ = states_ref.shape
    per = p_ref.shape[1] // n
    begin = RIM + mine_ref[1] * per
    p = p_ref[...]
    for v in range(channels):
        out_ref[v] = states_ref[v].astype(F32) + mixed(states_ref, tall_ref, v, p, [begin + g for g in range(per)])


def rest_kernel(mine_ref, p_ref, states_ref, tall_ref, acc_ref, out_ref):
    channels, n, _ = states_ref.shape
    per = p_ref.shape[2] // n
    order = [lax.rem(mine_ref[1] + d, SPAN) for d in range(1, SPAN)]
    p = jnp.concatenate([p_ref[i] for i in order], axis=1)
    slots = [RIM + i * per + g for i in order for g in range(per)]
    for v in range(channels):
        out_ref[v] = acc_ref[v] + mixed(states_ref, tall_ref, v, p, slots)


def halo_kernel(odd_ref, mate_ref, other_ref, states_ref, tall_ref, acc_ref, out_ref, rows, made, sems):
    channels, n, points = states_ref.shape
    last = tall_ref.shape[0]
    slots = [*range(RIM), *range(last - RIM, last)]
    odd = odd_ref[0] == 1
    low = jnp.where(odd, mate_ref[...], other_ref[...])
    high = jnp.where(odd, other_ref[...], mate_ref[...])
    p = jnp.concatenate([low, high], axis=1)
    copies = []
    for begin in range(0, points, 2 * LANES):
        for v in range(channels):
            acc = acc_ref[v, :, begin : begin + 2 * LANES]
            acc = acc + mixed(states_ref, tall_ref, v, p, slots, begin, 2 * LANES)
            for t in range(2):
                rows[t, pl.ds(v, n, stride=channels), :] = acc[:, t * LANES : (t + 1) * LANES]
        for t in range(2):
            at = slice(begin + t * LANES, begin + (t + 1) * LANES)
            for i in range(n):
                made[i, :, at] = rows[t, i * channels : (i + 1) * channels, :].astype(BF16)
        at = pl.ds(begin, 2 * LANES)
        copy = pltpu.make_async_copy(made.at[:, :, at], out_ref.at[:, :, at], sems.at[len(copies)])
        copy.start()
        copies.append(copy)
    for copy in copies:
        copy.wait()


def call(body, outs, *operands, scratch=(), scalars=0, flops=None):
    vmem = pl.BlockSpec(memory_space=pltpu.VMEM)
    smem = pl.BlockSpec(memory_space=pltpu.SMEM)
    held = [
        x[0] if isinstance(x, tuple) else pltpu.with_memory_space_constraint(x, pltpu.VMEM) for x in operands[scalars:]
    ]
    cost = None if flops is None else pl.CostEstimate(flops=flops, bytes_accessed=0, transcendentals=0)
    return pl.pallas_call(
        body,
        out_shape=outs,
        in_specs=[smem] * scalars + [vmem] * len(held),
        out_specs=jax.tree.map(
            lambda out: pl.BlockSpec(memory_space=pltpu.HBM) if isinstance(out, jax.ShapeDtypeStruct) else vmem,
            outs,
            is_leaf=lambda x: not isinstance(x, (list, tuple)),
        ),
        scratch_shapes=list(scratch),
        compiler_params=pltpu.CompilerParams(vmem_limit_bytes=40 * 1024 * 1024),
        cost_estimate=cost,
        name=body.__name__.removesuffix("_kernel"),
    )(*operands[:scalars], *held)


def on_device(weight_change, ensemble, stencil_index, stencil_weight):
    _, n, _, cols = weight_change.shape
    per = cols // SPAN
    lanes = per * n
    shape = jax.ShapeDtypeStruct
    raw = jnp.transpose(weight_change[0], (0, 2, 1))
    states = ensemble[0]
    _, channels, points = states.shape
    slots = cols + 2 * RIM
    rows = pltpu.VMEM((points // LANES, n * channels, LANES), F32)

    chunk = pltpu.VMEM((n, lanes), BF16)
    chunks = pltpu.VMEM((SPAN, n, lanes), BF16)
    packed = call(pack_kernel, chunks, (raw,), scratch=[pltpu.VMEM((n * cols, LANES), F32)])
    days = lax.all_to_all(packed, "cyc", 0, 0, axis_index_groups=NEAR, tiled=True)
    flat, tall = call(
        ready_kernel,
        (pltpu.VMEM((channels, n, points), BF16), pltpu.VMEM((slots, 16, points), BF16)),
        (stencil_index,),
        (stencil_weight,),
        (states,),
        scratch=[rows],
        flops=400_000_000,
    )
    near, whole = call(near_kernel, (pltpu.VMEM((SPAN - 1, n, lanes), BF16), chunk), days)
    wholes = lax.all_gather(whole, "cyc", axis=0, axis_index_groups=FAR)
    place = lax.axis_index("cyc").astype(jnp.int32)
    mine = jnp.stack([place // SPAN, place % SPAN])
    sent, own = call(
        far_kernel,
        (shape((SPAN, n, lanes), BF16), chunk),
        mine,
        wholes,
        near,
        scratch=[chunks, pltpu.SemaphoreType.DMA((SPAN,))],
        scalars=1,
    )
    suffix = lax.all_to_all(sent, "cyc", 0, 0, axis_index_groups=NEAR, tiled=True)
    count = lax.axis_size("tile")
    odd = lax.axis_index("tile").astype(jnp.int32) % 2
    first, last = suffix[0, :, : RIM * n], suffix[SPAN - 1, :, lanes - RIM * n :]
    others = [(i, (i - 1 + 2 * (i % 2)) % count) for i in range(count)]
    mates = [(i, i + 1 - 2 * (i % 2)) for i in range(count)]
    other = lax.ppermute(jnp.where(odd == 1, last, first), "tile", others)
    mate = lax.ppermute(jnp.where(odd == 1, first, last), "tile", mates)
    sums = pltpu.VMEM((channels, n, points), F32)
    acc = call(own_kernel, sums, mine, own, flat, tall, scalars=1, flops=420_000_000)
    acc = call(rest_kernel, sums, mine, suffix, flat, tall, acc, scalars=1, flops=1_260_000_000)
    result = call(
        halo_kernel,
        shape(states.shape, BF16),
        odd.reshape(1),
        mate,
        other,
        flat,
        tall,
        acc,
        scratch=[
            pltpu.VMEM((2, n * channels, LANES), F32),
            pltpu.VMEM(states.shape, BF16),
            pltpu.SemaphoreType.DMA((points // LANES // 2,)),
        ],
        scalars=1,
    )
    return result[None]


def solution(mesh):
    placed = (
        P("cyc", None, None, "tile"),
        P("cyc", None, None, "tile"),
        P(None, "tile"),
        P(None, "tile"),
    )
    return jax.shard_map(
        on_device,
        mesh=mesh,
        in_specs=placed,
        out_specs=P("cyc", None, None, "tile"),
        check_vma=False,
    )
```

time: 92.6 us -> 77.8 us (0.84)
  the two profiles are of different devices: /device:TPU:32 before, /device:TPU:31 now
where the time goes in v2:
time: 77.8 us; the launch traced here: 77.5 us
  blocking collectives  25.3 us (33%)
  waiting for transfers between devices  20.6 us (26%)
  starting transfers between devices  18.2 us (23%)
  Pallas kernels  12 us (15%)
  local copies, waits for them, and re-layouts  1.1 us (1%)
    all_gather x1, blocking collectives, on_device(): wholes = lax.all_gather(whole, 'cyc', axis=0, axis_index_groups=FAR)  25.3 us
    pallas_call x7, Pallas kernels, call(): pl.pallas_call(body, out_shape=outs, in_specs=[smem] * scalars + [vmem] *...  12 us
    all_to_all x1, waiting for transfers between devices, on_device(): lax.all_to_all(packed, 'cyc', 0, 0, axis_index_groups=NEAR, tiled=True)  11.5 us
    ppermute x1, starting transfers between devices, on_device(): mate = lax.ppermute(jnp.where(odd == 1, first, last), 'tile', mates)  7.05 us
    all_to_all x1, waiting for transfers between devices, on_device(): lax.all_to_all(sent, 'cyc', 0, 0, axis_index_groups=NEAR, tiled=True)  5.85 us
    all_to_all x1, starting transfers between devices, on_device(): lax.all_to_all(packed, 'cyc', 0, 0, axis_index_groups=NEAR, tiled=True)  5.61 us
    all_to_all x1, starting transfers between devices, on_device(): lax.all_to_all(sent, 'cyc', 0, 0, axis_index_groups=NEAR, tiled=True)  3.47 us
    ppermute x1, waiting for transfers between devices, on_device(): other = lax.ppermute(jnp.where(odd == 1, last, first), 'tile', others)  3.25 us
  transfers between devices with their start and end apart: 4, of which 3 were waited for; matrix products, arithmetic and copies ran while one was open for 0% of the time, Pallas kernels for 7%

profile of v2, /device:TPU:31, one launch (start us, length us, event | category | flops | bytes accessed | tf_op | source)
XLA Modules:
  0.0 77.5 jit_solution(5271596728757399427)
XLA Ops:
  0.0 0.0 copy-start
  0.0 1.1 %copy-done = bf16[1,80,80,32]{2,3,1,0:T(8,128)(2,1)S(1)} copy-done((bf16[1,80,80,32]{2,3,1,0:T(8,128)(2,1)S(1)}, bf16[1,80,80,32]{2,3,1,0:T(8,128)(2,1)}, u32[]{:S(2)}) %copy-start) | copy-done | bytes 409624
  1.1 1.8 %pack.1 = bf16[4,80,640]{2,1,0:T(8,128)(2,1)} custom-call(bf16[80,32,80]{2,1,0:T(8,128)(2,1)S(1)} %bitcast.14), custom_call_target="tpu_custom_call" | custom-call | tf_op jit(solution)/shard_map/pack/pallas_call | solution.py:176
  2.9 5.6 %all-to-all-start = ((bf16[4,80,640]{2,1,0:T(8,128)(2,1)}), bf16[4,80,640]{2,1,0:T(8,128)(2,1)S(1)}, u32[]{:S(2)}, u32[]{:S(2)}) async-start(bf16[4,80,640]{2,1,0:T(8,128)(2,1)} %pack.1), calls=%async_computation | async-start | bytes 819200 | tf_op jit(solution)/shard_map/all_to_all | solution.py:206
  8.5 0.0 copy-start.1
  8.5 0.0 copy-start.2
  8.5 0.0 copy-start.3
  8.5 0.1 pad_add_fusion.mine_ref
  8.6 11.5 %all-to-all-done.d_ref = bf16[4,80,640]{2,1,0:T(8,128)(2,1)S(1)} async-done(((bf16[4,80,640]{2,1,0:T(8,128)(2,1)}), bf16[4,80,640]{2,1,0:T(8,128)(2,1)S(1)}, u32[]{:S(2)}, u32[]{:S(2)}) %all-to-all-start) | async-done | bytes 409632 | tf_op jit(solution)/shard_map/all_to_all | solution.py:206
  20.1 0.7 near.1
  20.8 25.3 %all-gather = bf16[320,640]{1,0:T(8,128)(2,1)S(1)} all-gather(bf16[80,640]{1,0:T(8,128)(2,1)S(1)} %get-tuple-element.11), channel_id=2, replica_groups={{0,128,256,384},{32,160,288,416},{64,192,320,448},{96,224,352,480},{1,1..., dimensions={0}, use_global_device_ids=true | all-gather | bytes 512000 | tf_op jit(solution)/shard_map/all_gather | solution.py:217
  46.1 2.1 %far.1 = (bf16[4,80,640]{2,1,0:T(8,128)(2,1)}, bf16[80,640]{1,0:T(8,128)(2,1)S(1)}) custom-call(s32[2]{0:T(128)S(1)} %pad_add_fusion.mine_ref, bf16[4,80,640]{2,1,0:T(8,128)(2,1)S(1)} %bitcast.13, bf16[3,80,640]{2,1,0:T(8,128)(2,1)S(1)} %get-tuple-element.12.e_ref), custom_call_target="tpu_custom_call" | custom-call | tf_op jit(solution)/shard_map/far/pallas_call | solution.py:176
  48.1 3.5 %all-to-all-start.1 = ((bf16[4,80,640]{2,1,0:T(8,128)(2,1)}), bf16[4,80,640]{2,1,0:T(8,128)(2,1)S(1)}, u32[]{:S(2)}, u32[]{:S(2)}) async-start(bf16[4,80,640]{2,1,0:T(8,128)(2,1)} %get-tuple-element.13), calls=%async_computation.1 | async-start | bytes 819200 | tf_op jit(solution)/shard_map/all_to_all | solution.py:229
  51.6 0.0 copy-done.1
  51.6 0.0 copy-done.2
  51.6 0.0 copy-done.3
  51.7 0.5 ready.1
  52.1 1.6 %own.1.acc_ref = f32[8,80,512]{2,1,0:T(8,128)S(1)} custom-call(s32[2]{0:T(128)S(1)} %pad_add_fusion.mine_ref, bf16[80,640]{1,0:T(8,128)(2,1)S(1)} %get-tuple-element.16.p_ref, bf16[8,80,512]{2,1,0:T(8,128)(2,1)S(1)} %get-tuple-element.14.states_ref, bf16[40,16,512]{2,1,0:T(8,128)(2,1)S(1)} %get-tuple-element.15.tall_ref), custom_call_target="tpu_custom_call" | custom-call | flops 420000000 | tf_op jit(solution)/shard_map/own/pallas_call | solution.py:176
  53.7 5.8 %all-to-all-done.1.p_ref = bf16[4,80,640]{2,1,0:T(8,128)(2,1)S(1)} async-done(((bf16[4,80,640]{2,1,0:T(8,128)(2,1)}), bf16[4,80,640]{2,1,0:T(8,128)(2,1)S(1)}, u32[]{:S(2)}, u32[]{:S(2)}) %all-to-all-start.1) | async-done | bytes 409632 | tf_op jit(solution)/shard_map/all_to_all | solution.py:229
  59.6 0.1 select_bitcast_fusion
  59.7 7.0 %collective-permute-start = (bf16[80,320]{1,0:T(8,128)(2,1)S(1)}, bf16[80,320]{1,0:T(8,128)(2,1)S(1)}, u32[]{:S(2)}, u32[]{:S(2)}) collective-permute-start(bf16[80,320]{1,0:T(8,128)(2,1)S(1)} %get-tuple-element.18), channel_id=1, source_target_pairs={{0,1},{1,0},{2,3},{3,2},{4,5},{5,4},{6,7},{7,6},{8,9},{9,8},{10,11... | collective-permute-start | bytes 153608 | tf_op jit(solution)/shard_map/ppermute | solution.py:236
  66.7 2.1 %collective-permute-start.1 = (bf16[80,320]{1,0:T(8,128)(2,1)S(1)}, bf16[80,320]{1,0:T(8,128)(2,1)S(1)}, u32[]{:S(2)}, u32[]{:S(2)}) collective-permute-start(bf16[80,320]{1,0:T(8,128)(2,1)S(1)} %get-tuple-element.17), channel_id=1, source_target_pairs={{0,31},{1,2},{2,1},{3,4},{4,3},{5,6},{6,5},{7,8},{8,7},{9,10},{10,... | collective-permute-start | bytes 153608 | tf_op jit(solution)/shard_map/ppermute | solution.py:235
  68.9 3.5 %rest.1.acc_ref = f32[8,80,512]{2,1,0:T(8,128)S(1)} custom-call(s32[2]{0:T(128)S(1)} %pad_add_fusion.mine_ref, bf16[4,80,640]{2,1,0:T(8,128)(2,1)S(1)} %all-to-all-done.1.p_ref, bf16[8,80,512]{2,1,0:T(8,128)(2,1)S(1)} %get-tuple-element.14.states_ref, bf16[40,16,512]{2,1,0:T(8,128)(2,1)S(1)} %get-tuple-element.15.tall_ref, f32[8,80,512]{2,1,0:T(8,128)S(1)} %own.1.acc_ref), custom_call_target="tpu_custom_call" | custom-call | flops 1260000000 | tf_op jit(solution)/shard_map/rest/pallas_call | solution.py:176
  72.3 0.0 collective-permute-done.mate_ref
  72.3 3.3 %collective-permute-done.1.other_ref = bf16[80,320]{1,0:T(8,128)(2,1)S(1)} collective-permute-done((bf16[80,320]{1,0:T(8,128)(2,1)S(1)}, bf16[80,320]{1,0:T(8,128)(2,1)S(1)}, u32[]{:S(2)}, u32[]{:S(2)}) %collective-permute-start.1) | collective-permute-done | bytes 51232 | tf_op jit(solution)/shard_map/ppermute | solution.py:235
  75.6 1.9 %halo.1 = bf16[80,8,512]{2,1,0:T(8,128)(2,1)} custom-call(s32[1]{0:T(128)} %bitcast.odd_ref, bf16[80,320]{1,0:T(8,128)(2,1)S(1)} %collective-permute-done.mate_ref, bf16[80,320]{1,0:T(8,128)(2,1)S(1)} %collective-permute-done.1.other_ref, bf16[8,80,512]{2,1,0:T(8,128)(2,1)S(1)} %get-tuple-element.14.states_ref, ...), custom_call_target="tpu_custom_call" | custom-call | tf_op jit(solution)/shard_map/halo/pallas_call | solution.py:176
Async XLA Ops:
  0.0 1.1 %copy-start = (bf16[1,80,80,32]{2,3,1,0:T(8,128)(2,1)S(1)}, bf16[1,80,80,32]{2,3,1,0:T(8,128)(2,1)}, u32[]{:S(2)}) copy-start(bf16[1,80,80,32]{2,3,1,0:T(8,128)(2,1)} %param.4) | copy-start | bytes 1228804
  2.9 17.2 %all-to-all-start = ((bf16[4,80,640]{2,1,0:T(8,128)(2,1)}), bf16[4,80,640]{2,1,0:T(8,128)(2,1)S(1)}, u32[]{:S(2)}, u32[]{:S(2)}) async-start(bf16[4,80,640]{2,1,0:T(8,128)(2,1)} %pack.1), calls=%async_computation | async-start | bytes 819200 | tf_op jit(solution)/shard_map/all_to_all | solution.py:206
  8.5 43.1 %copy-start.1 = (bf16[1,80,8,512]{3,2,1,0:T(8,128)(2,1)S(1)}, bf16[1,80,8,512]{3,2,1,0:T(8,128)(2,1)}, u32[]{:S(2)}) copy-start(bf16[1,80,8,512]{3,2,1,0:T(8,128)(2,1)} %param.5) | copy-start | bytes 1966084
  8.5 43.1 %copy-start.2 = (s32[4,512]{1,0:T(4,128)S(1)}, s32[4,512]{1,0:T(4,128)}, u32[]{:S(2)}) copy-start(s32[4,512]{1,0:T(4,128)} %index_ref.1) | copy-start | bytes 24580
  8.5 43.1 %copy-start.3 = (f32[4,512]{1,0:T(4,128)S(1)}, f32[4,512]{1,0:T(4,128)}, u32[]{:S(2)}) copy-start(f32[4,512]{1,0:T(4,128)} %weight_ref.1) | copy-start | bytes 24580
  48.1 11.5 %all-to-all-start.1 = ((bf16[4,80,640]{2,1,0:T(8,128)(2,1)}), bf16[4,80,640]{2,1,0:T(8,128)(2,1)S(1)}, u32[]{:S(2)}, u32[]{:S(2)}) async-start(bf16[4,80,640]{2,1,0:T(8,128)(2,1)} %get-tuple-element.13), calls=%async_computation.1 | async-start | bytes 819200 | tf_op jit(solution)/shard_map/all_to_all | solution.py:229
  59.7 12.7 %collective-permute-start = (bf16[80,320]{1,0:T(8,128)(2,1)S(1)}, bf16[80,320]{1,0:T(8,128)(2,1)S(1)}, u32[]{:S(2)}, u32[]{:S(2)}) collective-permute-start(bf16[80,320]{1,0:T(8,128)(2,1)S(1)} %get-tuple-element.18), channel_id=1, source_target_pairs={{0,1},{1,0},{2,3},{3,2},{4,5},{5,4},{6,7},{7,6},{8,9},{9,8},{10,11... | collective-permute-start | bytes 153608 | tf_op jit(solution)/shard_map/ppermute | solution.py:236
  66.7 8.9 %collective-permute-start.1 = (bf16[80,320]{1,0:T(8,128)(2,1)S(1)}, bf16[80,320]{1,0:T(8,128)(2,1)S(1)}, u32[]{:S(2)}, u32[]{:S(2)}) collective-permute-start(bf16[80,320]{1,0:T(8,128)(2,1)S(1)} %get-tuple-element.17), channel_id=1, source_target_pairs={{0,31},{1,2},{2,1},{3,4},{4,3},{5,6},{6,5},{7,8},{8,7},{9,10},{10,... | collective-permute-start | bytes 153608 | tf_op jit(solution)/shard_map/ppermute | solution.py:235

commit v3 on v2

--- a/solution.py
+++ b/solution.py
@@ -64,24 +64,17 @@
     g_ref[...] = joined(e0, d0).astype(BF16)
 
 
-def far_kernel(mine_ref, w_ref, e_ref, out_ref, own_ref, made, sems):
+def far_kernel(mine_ref, w_ref, e_ref, out_ref):
     mine = mine_ref[0]
-    place = mine_ref[1]
     _, h1, h2, h3 = [w_ref[k] * jnp.where(mine < k, 1.0, 0.0).astype(BF16) for k in range(SPAN)]
     s = joined(h3.astype(F32) + h2.astype(F32) + product(h3, h2), h1)
     n = s.shape[0]
     parts = halves(s)
-    copies = [pltpu.make_async_copy(made.at[r], out_ref.at[r], sems.at[r]) for r in range(SPAN)]
-    made[SPAN - 1] = s.astype(BF16)
-    copies[SPAN - 1].start()
+    out_ref[SPAN - 1] = s.astype(BF16)
     for r in range(SPAN - 1):
         e = e_ref[r]
         both = product(parts, e)
-        made[r] = (s + e.astype(F32) + both[:n] + both[n:]).astype(BF16)
-        copies[r].start()
-    own_ref[...] = made[place]
-    for copy in copies:
-        copy.wait()
+        out_ref[r] = (s + e.astype(F32) + both[:n] + both[n:]).astype(BF16)
 
 
 def table_of(index_ref, weight_ref, slots):
@@ -120,23 +113,13 @@
     return mm(matrices, many)
 
 
-def own_kernel(mine_ref, p_ref, states_ref, tall_ref, out_ref):
+def local_kernel(p_ref, states_ref, tall_ref, out_ref):
     channels, n, _ = states_ref.shape
-    per = p_ref.shape[1] // n
-    begin = RIM + mine_ref[1] * per
-    p = p_ref[...]
+    chunks = p_ref.shape[0]
+    slots = range(RIM, RIM + chunks * (p_ref.shape[2] // n))
+    p = jnp.concatenate([p_ref[i] for i in range(chunks)], axis=1)
     for v in range(channels):
-        out_ref[v] = states_ref[v].astype(F32) + mixed(states_ref, tall_ref, v, p, [begin + g for g in range(per)])
-
-
-def rest_kernel(mine_ref, p_ref, states_ref, tall_ref, acc_ref, out_ref):
-    channels, n, _ = states_ref.shape
-    per = p_ref.shape[2] // n
-    order = [lax.rem(mine_ref[1] + d, SPAN) for d in range(1, SPAN)]
-    p = jnp.concatenate([p_ref[i] for i in order], axis=1)
-    slots = [RIM + i * per + g for i in order for g in range(per)]
-    for v in range(channels):
-        out_ref[v] = acc_ref[v] + mixed(states_ref, tall_ref, v, p, slots)
+        out_ref[v] = states_ref[v].astype(F32) + mixed(states_ref, tall_ref, v, p, slots)
 
 
 def halo_kernel(odd_ref, mate_ref, other_ref, states_ref, tall_ref, acc_ref, out_ref, rows, made, sems):
@@ -202,6 +185,10 @@
 
     chunk = pltpu.VMEM((n, lanes), BF16)
     chunks = pltpu.VMEM((SPAN, n, lanes), BF16)
+    place = lax.axis_index("cyc").astype(jnp.int32)
+    sector = lax.axis_index("tile").astype(jnp.int32)
+    mine = jnp.stack([place // SPAN, place % SPAN])
+    raw, mine, odd, is_odd = lax.optimization_barrier((raw, mine, (sector % 2).reshape(1), sector % 2 == 1))
     packed = call(pack_kernel, chunks, (raw,), scratch=[pltpu.VMEM((n * cols, LANES), F32)])
     days = lax.all_to_all(packed, "cyc", 0, 0, axis_index_groups=NEAR, tiled=True)
     flat, tall = call(
@@ -213,34 +200,23 @@
         scratch=[rows],
         flops=400_000_000,
     )
+    days, flat, tall = lax.optimization_barrier((days, flat, tall))
     near, whole = call(near_kernel, (pltpu.VMEM((SPAN - 1, n, lanes), BF16), chunk), days)
     wholes = lax.all_gather(whole, "cyc", axis=0, axis_index_groups=FAR)
-    place = lax.axis_index("cyc").astype(jnp.int32)
-    mine = jnp.stack([place // SPAN, place % SPAN])
-    sent, own = call(
-        far_kernel,
-        (shape((SPAN, n, lanes), BF16), chunk),
-        mine,
-        wholes,
-        near,
-        scratch=[chunks, pltpu.SemaphoreType.DMA((SPAN,))],
-        scalars=1,
-    )
+    sent = call(far_kernel, chunks, mine, wholes, near, scalars=1)
     suffix = lax.all_to_all(sent, "cyc", 0, 0, axis_index_groups=NEAR, tiled=True)
     count = lax.axis_size("tile")
-    odd = lax.axis_index("tile").astype(jnp.int32) % 2
     first, last = suffix[0, :, : RIM * n], suffix[SPAN - 1, :, lanes - RIM * n :]
     others = [(i, (i - 1 + 2 * (i % 2)) % count) for i in range(count)]
     mates = [(i, i + 1 - 2 * (i % 2)) for i in range(count)]
-    other = lax.ppermute(jnp.where(odd == 1, last, first), "tile", others)
-    mate = lax.ppermute(jnp.where(odd == 1, first, last), "tile", mates)
+    other = lax.ppermute(jnp.where(is_odd, last, first), "tile", others)
+    mate = lax.ppermute(jnp.where(is_odd, first, last), "tile", mates)
     sums = pltpu.VMEM((channels, n, points), F32)
-    acc = call(own_kernel, sums, mine, own, flat, tall, scalars=1, flops=420_000_000)
-    acc = call(rest_kernel, sums, mine, suffix, flat, tall, acc, scalars=1, flops=1_260_000_000)
+    acc = call(local_kernel, sums, suffix, flat, tall, flops=1_680_000_000)
     result = call(
         halo_kernel,
         shape(states.shape, BF16),
-        odd.reshape(1),
+        odd,
         mate,
         other,
         flat,

time: 77.8 us -> 75.9 us (0.976)
  the two profiles are of different devices: /device:TPU:31 before, /device:TPU:1 now
where the time goes in v3:
time: 75.9 us; the launch traced here: 75.7 us
  blocking collectives  39.2 us (52%)
  starting transfers between devices  17.7 us (23%)
  Pallas kernels  9.96 us (13%)
  waiting for transfers between devices  7.5 us (10%)
  local copies, waits for them, and re-layouts  1.1 us (1%)
    all_gather x1, blocking collectives, on_device(): wholes = lax.all_gather(whole, 'cyc', axis=0, axis_index_groups=FAR)  28.9 us
    all_to_all x1, blocking collectives, on_device(): lax.all_to_all(sent, 'cyc', 0, 0, axis_index_groups=NEAR, tiled=True)  10.3 us
    pallas_call x6, Pallas kernels, call(): pl.pallas_call(body, out_shape=outs, in_specs=[smem] * scalars + [vmem] *...  9.96 us
    ppermute x1, starting transfers between devices, on_device(): other = lax.ppermute(jnp.where(is_odd, last, first), 'tile', others)  9.37 us
    all_to_all x1, waiting for transfers between devices, on_device(): lax.all_to_all(packed, 'cyc', 0, 0, axis_index_groups=NEAR, tiled=True)  7.49 us
    all_to_all x1, starting transfers between devices, on_device(): lax.all_to_all(packed, 'cyc', 0, 0, axis_index_groups=NEAR, tiled=True)  6.43 us
    ppermute x1, starting transfers between devices, on_device(): mate = lax.ppermute(jnp.where(is_odd, first, last), 'tile', mates)  1.92 us
  transfers between devices with their start and end apart: 3, of which 1 were waited for; matrix products, arithmetic and copies ran while one was open for 0% of the time, Pallas kernels for 6%

profile of v3, /device:TPU:1, one launch (start us, length us, event | category | flops | bytes accessed | tf_op | source)
XLA Modules:
  0.0 75.7 jit_solution(7121192929159819677)
XLA Ops:
  0.0 0.0 copy-start.3
  0.0 0.0 copy-start.2
  0.0 0.1 pad_add_fusion.mine_ref
  0.1 0.0 copy-start
  0.1 1.1 %copy-done = bf16[1,80,80,32]{2,3,1,0:T(8,128)(2,1)S(1)} copy-done((bf16[1,80,80,32]{2,3,1,0:T(8,128)(2,1)S(1)}, bf16[1,80,80,32]{2,3,1,0:T(8,128)(2,1)}, u32[]{:S(2)}) %copy-start) | copy-done | bytes 409624
  1.2 0.0 copy-start.1
  1.2 1.8 %pack.1 = bf16[4,80,640]{2,1,0:T(8,128)(2,1)} custom-call(bf16[80,32,80]{2,1,0:T(8,128)(2,1)S(1)} %bitcast.14), custom_call_target="tpu_custom_call" | custom-call | tf_op jit(solution)/shard_map/pack/pallas_call | solution.py:159
  3.0 6.4 %all-to-all-start = ((bf16[4,80,640]{2,1,0:T(8,128)(2,1)}), bf16[4,80,640]{2,1,0:T(8,128)(2,1)S(1)}, u32[]{:S(2)}, u32[]{:S(2)}) async-start(bf16[4,80,640]{2,1,0:T(8,128)(2,1)} %pack.1), calls=%async_computation | async-start | bytes 819200 | tf_op jit(solution)/shard_map/all_to_all | solution.py:193
  9.4 0.0 copy-done.3
  9.4 0.0 copy-done.2
  9.4 0.0 copy-done.1
  9.4 0.5 ready.1
  9.9 7.5 %all-to-all-done.d_ref = bf16[4,80,640]{2,1,0:T(8,128)(2,1)S(1)} async-done(((bf16[4,80,640]{2,1,0:T(8,128)(2,1)}), bf16[4,80,640]{2,1,0:T(8,128)(2,1)S(1)}, u32[]{:S(2)}, u32[]{:S(2)}) %all-to-all-start) | async-done | bytes 409632 | tf_op jit(solution)/shard_map/all_to_all | solution.py:193
  17.4 0.7 near.1
  18.0 28.9 %all-gather = bf16[320,640]{1,0:T(8,128)(2,1)S(1)} all-gather(bf16[80,640]{1,0:T(8,128)(2,1)S(1)} %get-tuple-element.23), channel_id=2, replica_groups={{0,128,256,384},{32,160,288,416},{64,192,320,448},{96,224,352,480},{1,1..., dimensions={0}, use_global_device_ids=true | all-gather | bytes 512000 | tf_op jit(solution)/shard_map/all_gather | solution.py:205
  46.9 1.4 %far.1 = bf16[4,80,640]{2,1,0:T(8,128)(2,1)S(1)} custom-call(s32[2]{0:T(128)S(1)} %pad_add_fusion.mine_ref, bf16[4,80,640]{2,1,0:T(8,128)(2,1)S(1)} %bitcast.13, bf16[3,80,640]{2,1,0:T(8,128)(2,1)S(1)} %get-tuple-element.24.e_ref), custom_call_target="tpu_custom_call" | custom-call | tf_op jit(solution)/shard_map/far/pallas_call | solution.py:159
  48.3 10.3 %all_to_all.10.p_ref = bf16[4,80,640]{2,1,0:T(8,128)(2,1)S(1)} all-to-all(bf16[4,80,640]{2,1,0:T(8,128)(2,1)S(1)} %far.1), channel_id=1, replica_groups={{0,32,64,96},{128,160,192,224},{256,288,320,352},{384,416,448,480},{1,3..., dimensions={0} | all-to-all | bytes 819200 | tf_op jit(solution)/shard_map/all_to_all | solution.py:207
  58.6 0.1 select_bitcast_fusion
  58.7 9.4 %collective-permute-start.1 = (bf16[80,320]{1,0:T(8,128)(2,1)S(1)}, bf16[80,320]{1,0:T(8,128)(2,1)S(1)}, u32[]{:S(2)}, u32[]{:S(2)}) collective-permute-start(bf16[80,320]{1,0:T(8,128)(2,1)S(1)} %get-tuple-element.27), channel_id=1, source_target_pairs={{0,31},{1,2},{2,1},{3,4},{4,3},{5,6},{6,5},{7,8},{8,7},{9,10},{10,... | collective-permute-start | bytes 153608 | tf_op jit(solution)/shard_map/ppermute | solution.py:212
  68.1 1.9 %collective-permute-start = (bf16[80,320]{1,0:T(8,128)(2,1)S(1)}, bf16[80,320]{1,0:T(8,128)(2,1)S(1)}, u32[]{:S(2)}, u32[]{:S(2)}) collective-permute-start(bf16[80,320]{1,0:T(8,128)(2,1)S(1)} %get-tuple-element.28), channel_id=1, source_target_pairs={{0,1},{1,0},{2,3},{3,2},{4,5},{5,4},{6,7},{7,6},{8,9},{9,8},{10,11... | collective-permute-start | bytes 153608 | tf_op jit(solution)/shard_map/ppermute | solution.py:213
  70.0 3.7 %local.1.acc_ref = f32[8,80,512]{2,1,0:T(8,128)S(1)} custom-call(bf16[4,80,640]{2,1,0:T(8,128)(2,1)S(1)} %all_to_all.10.p_ref, bf16[8,80,512]{2,1,0:T(8,128)(2,1)S(1)} %get-tuple-element.25.states_ref, bf16[40,16,512]{2,1,0:T(8,128)(2,1)S(1)} %get-tuple-element.26.tall_ref), custom_call_target="tpu_custom_call" | custom-call | flops 1680000000 | tf_op jit(solution)/shard_map/local/pallas_call | solution.py:159
  73.7 0.0 collective-permute-done.1.other_ref
  73.7 0.0 collective-permute-done.mate_ref
  73.7 1.9 %halo.1 = bf16[80,8,512]{2,1,0:T(8,128)(2,1)} custom-call(s32[1]{0:T(128)} %bitcast.4.odd_ref, bf16[80,320]{1,0:T(8,128)(2,1)S(1)} %collective-permute-done.mate_ref, bf16[80,320]{1,0:T(8,128)(2,1)S(1)} %collective-permute-done.1.other_ref, bf16[8,80,512]{2,1,0:T(8,128)(2,1)S(1)} %get-tuple-element.25.states_ref, ...), custom_call_target="tpu_custom_call" | custom-call | tf_op jit(solution)/shard_map/halo/pallas_call | solution.py:159
Async XLA Ops:
  0.0 9.4 %copy-start.3 = (f32[4,512]{1,0:T(4,128)S(1)}, f32[4,512]{1,0:T(4,128)}, u32[]{:S(2)}) copy-start(f32[4,512]{1,0:T(4,128)} %weight_ref.1) | copy-start | bytes 24580
  0.0 9.4 %copy-start.2 = (s32[4,512]{1,0:T(4,128)S(1)}, s32[4,512]{1,0:T(4,128)}, u32[]{:S(2)}) copy-start(s32[4,512]{1,0:T(4,128)} %index_ref.1) | copy-start | bytes 24580
  0.1 1.1 %copy-start = (bf16[1,80,80,32]{2,3,1,0:T(8,128)(2,1)S(1)}, bf16[1,80,80,32]{2,3,1,0:T(8,128)(2,1)}, u32[]{:S(2)}) copy-start(bf16[1,80,80,32]{2,3,1,0:T(8,128)(2,1)} %param.4) | copy-start | bytes 1228804
  1.2 8.2 %copy-start.1 = (bf16[1,80,8,512]{3,2,1,0:T(8,128)(2,1)S(1)}, bf16[1,80,8,512]{3,2,1,0:T(8,128)(2,1)}, u32[]{:S(2)}) copy-start(bf16[1,80,8,512]{3,2,1,0:T(8,128)(2,1)} %param.5) | copy-start | bytes 1966084
  3.0 14.4 %all-to-all-start = ((bf16[4,80,640]{2,1,0:T(8,128)(2,1)}), bf16[4,80,640]{2,1,0:T(8,128)(2,1)S(1)}, u32[]{:S(2)}, u32[]{:S(2)}) async-start(bf16[4,80,640]{2,1,0:T(8,128)(2,1)} %pack.1), calls=%async_computation | async-start | bytes 819200 | tf_op jit(solution)/shard_map/all_to_all | solution.py:193
  58.7 15.0 %collective-permute-start.1 = (bf16[80,320]{1,0:T(8,128)(2,1)S(1)}, bf16[80,320]{1,0:T(8,128)(2,1)S(1)}, u32[]{:S(2)}, u32[]{:S(2)}) collective-permute-start(bf16[80,320]{1,0:T(8,128)(2,1)S(1)} %get-tuple-element.27), channel_id=1, source_target_pairs={{0,31},{1,2},{2,1},{3,4},{4,3},{5,6},{6,5},{7,8},{8,7},{9,10},{10,... | collective-permute-start | bytes 153608 | tf_op jit(solution)/shard_map/ppermute | solution.py:212
  68.1 5.7 %collective-permute-start = (bf16[80,320]{1,0:T(8,128)(2,1)S(1)}, bf16[80,320]{1,0:T(8,128)(2,1)S(1)}, u32[]{:S(2)}, u32[]{:S(2)}) collective-permute-start(bf16[80,320]{1,0:T(8,128)(2,1)S(1)} %get-tuple-element.28), channel_id=1, source_target_pairs={{0,1},{1,0},{2,3},{3,2},{4,5},{5,4},{6,7},{7,6},{8,9},{9,8},{10,11... | collective-permute-start | bytes 153608 | tf_op jit(solution)/shard_map/ppermute | solution.py:213
